TPU v7x, 32 devices: a whole 2x2x4 slice. The times are simulated.
32 devices in a mesh: gx: 16 (over z, y, core), gy: 2 (over x).
Axes of the slice: x: 2, y: 2, z: 4, core: 2. Of those that a mesh axis runs over, the one named last changes fastest.
Arguments:
- right_side: float32 [16, 2, 512, 256], P('gx', 'gy'), may hold values from -8 to 8, as said below
- coords: float32 [16, 2, 2, 512], P('gx', 'gy'), may hold values from 0 to 1
- noise: float32 [16, 2, 512], P('gx', 'gy'), may hold values from 0.25 to 1
- intersect: int32 [16, 2, 128], P('gx', 'gy'), may hold values from 0 to 4607, as said below
Outputs:
- solution: float32 [16, 2, 512, 256], P('gx', 'gy')
- residual: float32 [16, 2, 512, 256], P('gx', 'gy')
Inputs may be any that keep to these rules, and one draw needn't show every extreme that they name: `right_side`: right-hand sides of order one. `intersect`: each subdomain's list holds 128 distinct indices in increasing order; none names the subdomain itself (block number 4) or a subdomain beyond the first or last one along the second dimension.
All inputs are finite; a program needn't handle non-finite values.
Results may differ from a plain program's by a relative error of at most 0.0003.
Values sent between devices are 32-bit elements; how exact they have to be, the bound alone decides.
A program may use at most 128 MiB of HBM per device.

v0:
```python
import math
import jax
import jax.numpy as jnp
from jax import lax
from jax.sharding import PartitionSpec as P

ITERS = 3
RANGE_LEN = 0.25
ROOT_THREE = math.sqrt(3.0)
HIGH = lax.Precision.HIGHEST


def shifted(value, axis, by):
    count = lax.axis_size(axis)
    return lax.ppermute(value, axis, [(i, (i + by) % count) for i in range(count)])


def passed_along(block, axis, distance):
    devices = range(lax.axis_size(axis))
    route = [(i - distance, i) for i in devices if i - distance in devices]
    return lax.ppermute(block, axis, route)


def kernel_block(rows_pos, cols_pos):
    delta_x = rows_pos[0][:, None] - cols_pos[0][None, :]
    delta_y = rows_pos[1][:, None] - cols_pos[1][None, :]
    distance = jnp.sqrt(delta_x * delta_x + delta_y * delta_y)
    scaled = ROOT_THREE / RANGE_LEN * distance
    clipped = jnp.minimum(distance, 1.0)
    taper_val = jnp.square(jnp.square(1.0 - clipped)) * (4.0 * clipped + 1.0)
    return (1.0 + scaled) * jnp.exp(-scaled) * taper_val


def window_values(values):
    beside = {}
    for step_by in (1, -1):
        beside[step_by] = shifted(values, "gx", step_by)
    column = jnp.stack([beside[1], values, beside[-1]])
    across = {}
    for step_by in (1, -1):
        across[step_by] = passed_along(column, "gy", step_by)
    return [across[1], column, across[-1]]


def window_index(values):
    beside = {}
    for step_by in (1, -1):
        beside[step_by] = shifted(values, "gx", step_by)
    column = jnp.stack([beside[1], values, beside[-1]])
    across = {}
    for step_by in (1, -1):
        across[step_by] = passed_along(column, "gy", step_by)
    return [across[1], column, across[-1]]


def column_sum(first, second):
    return jnp.sum(first * second, axis=0)


def residual_dot(residue, precond):
    return lax.psum(column_sum(residue, precond), ("gx", "gy"))


def shards(right_side, coords, noise, intersect):
    points = right_side.shape[2]
    rhs_count = right_side.shape[3]
    intersect_len = intersect.shape[2]
    ext_len = points + intersect_len
    own_pos = coords.reshape(2, points)
    own_noise = noise.reshape(points)
    point_info = jnp.concatenate([own_pos, own_noise[None, :]], axis=0)
    info_cols = window_values(point_info)
    positions = [
        [
            jnp.stack(
                [
                    info_cols[col_off][row_off, 0] + float(row_off - 1),
                    info_cols[col_off][row_off, 1] + float(col_off - 1),
                ]
            )
            for col_off in range(3)
        ]
        for row_off in range(3)
    ]
    intersect_ids = intersect.reshape(intersect_len)
    block_id = intersect_ids // points
    row_in = intersect_ids % points
    row_of = block_id // 3
    col_of = block_id % 3
    local_id = row_of * points + row_in
    picked_info = [
        jnp.take(
            jnp.transpose(info_cols[col_off], (1, 0, 2)).reshape(3, 3 * points), local_id, axis=1
        )
        for col_off in range(3)
    ]
    chosen = jnp.where(
        col_of[None, :] == 0,
        picked_info[0],
        jnp.where(col_of[None, :] == 1, picked_info[1], picked_info[2]),
    )
    ov_pos = jnp.stack(
        [chosen[0] + (row_of - 1).astype(jnp.float32), chosen[1] + (col_of - 1).astype(jnp.float32)]
    )
    ext_pos = jnp.concatenate([own_pos, ov_pos], axis=1)
    ext_noise = jnp.concatenate([own_noise, chosen[2]])
    local_matrix = kernel_block(ext_pos, ext_pos) + jnp.diag(ext_noise)
    factor = jnp.linalg.cholesky(local_matrix)
    inv_factor = lax.linalg.triangular_solve(
        factor, jnp.eye(ext_len, dtype=jnp.float32), left_side=True, lower=True
    )
    inverse = jnp.dot(inv_factor.T, inv_factor, precision=HIGH, preferred_element_type=jnp.float32)
    near_ids = window_index(intersect_ids)
    point_iota = jnp.arange(points, dtype=jnp.int32)[:, None]
    row_base = (2 - jnp.arange(3, dtype=jnp.int32))[:, None] * 3
    selectors = []
    for col_off in range(3):
        own_rows = near_ids[col_off] - (row_base + (2 - col_off)) * points
        selectors.append((point_iota == own_rows.reshape(1, 3 * intersect_len)).astype(jnp.float32))

    def borrowed_rows(residue):
        requested = [
            lax.dot_general(
                selectors[col_off],
                residue,
                (((0,), (0,)), ((), ())),
                precision=HIGH,
                preferred_element_type=jnp.float32,
            ).reshape(3, intersect_len, rhs_count)
            for col_off in range(3)
        ]
        combined = jnp.stack([requested[col_off][1] for col_off in range(3)])
        for step_by, row_off in ((-1, 0), (1, 2)):
            outgoing = jnp.stack([requested[col_off][row_off] for col_off in range(3)])
            combined = combined + shifted(outgoing, "gx", step_by)
        gathered = combined[1]
        for step_by, col_off in ((-1, 0), (1, 2)):
            gathered = gathered + passed_along(combined[col_off], "gy", step_by)
        return gathered

    def precondition(residue):
        gathered = borrowed_rows(residue)
        extended = jnp.concatenate([residue, gathered], axis=0)
        solved = jnp.dot(inverse, extended, precision=HIGH, preferred_element_type=jnp.float32)
        returned = window_values(solved[points:])
        result = solved[:points]
        for col_off in range(3):
            result = result + jnp.dot(
                selectors[col_off],
                returned[col_off].reshape(3 * intersect_len, rhs_count),
                precision=HIGH,
                preferred_element_type=jnp.float32,
            )
        return result

    noise_col = own_noise[:, None]
    residual = right_side.reshape(points, rhs_count)
    solution = jnp.zeros_like(residual)
    precond = precondition(residual)
    direction = precond
    inner_now = residual_dot(residual, precond)
    for iteration in range(ITERS):
        columns = window_values(direction)
        accumulated = noise_col * direction
        for operate_row_off in range(3):
            for operate_col_off in range(3):
                accumulated = accumulated + jnp.dot(
                    kernel_block(own_pos, positions[operate_row_off][operate_col_off]),
                    columns[operate_col_off][operate_row_off],
                    precision=HIGH,
                    preferred_element_type=jnp.float32,
                )
        step_size = inner_now / lax.psum(column_sum(direction, accumulated), ("gx", "gy"))
        solution = solution + step_size * direction
        residual = residual - step_size * accumulated
        if iteration + 1 < ITERS:
            precond = precondition(residual)
            inner_next = residual_dot(residual, precond)
            direction = precond + inner_next / inner_now * direction
            inner_now = inner_next
    return (solution.reshape(1, 1, points, rhs_count), residual.reshape(1, 1, points, rhs_count))


def solution(mesh):
    placed = (
        P("gx", "gy", None, None),
        P("gx", "gy", None, None),
        P("gx", "gy", None),
        P("gx", "gy", None),
    )
    return jax.shard_map(
        shards,
        mesh=mesh,
        in_specs=placed,
        out_specs=(P("gx", "gy", None, None), P("gx", "gy", None, None)),
        check_vma=False,
    )
```

profile of v0, /device:TPU:0, one launch (start us, length us, event | category | flops | bytes accessed | tf_op | source)
XLA Modules:
  0.0 750.6 jit_solution(9324209336027450057)
XLA Ops:
  1.2 5.0 collective-permute-start.5
  7.0 4.4 collective-permute-start.1
  15.4 4.5 collective-permute-start.6
  23.5 3.7 collective-permute-start.2
  34.4 3.1 add_multiply_fusion
  38.7 11.7 %cholesky.132 = f32[128,128]{1,0:T(8,128)S(1)} custom-call(f32[128,128]{1,0:T(8,128)S(1)} %cholesky.337), custom_call_target="Cholesky" | custom-call | tf_op jit(solution)/shard_map/jit(cholesky)/cholesky | solution.py:108
  50.6 9.8 %custom-call.38 = f32[1,128,128]{1,2,0:T(8,128)S(1)} custom-call(f32[1,128,128]{2,1,0:T(8,128)S(1)} %get-tuple-element.83), custom_call_target="InvertDiagBlocksLowerTriangular" | custom-call | tf_op jit(solution)/shard_map/jit(cholesky)/cholesky | solution.py:108
  63.0 11.9 %cholesky.270 = f32[128,128]{1,0:T(8,128)S(1)} custom-call(f32[128,128]{1,0:T(8,128)S(1)} %cholesky.341), custom_call_target="Cholesky" | custom-call | tf_op jit(solution)/shard_map/jit(cholesky)/cholesky | solution.py:108
  76.3 9.8 %custom-call.39 = f32[1,128,128]{1,2,0:T(8,128)S(1)} custom-call(f32[1,128,128]{2,1,0:T(8,128)S(1)} %get-tuple-element.80), custom_call_target="InvertDiagBlocksLowerTriangular" | custom-call | tf_op jit(solution)/shard_map/jit(cholesky)/cholesky | solution.py:108
  87.8 11.7 %cholesky.291 = f32[128,128]{1,0:T(8,128)S(1)} custom-call(f32[128,128]{1,0:T(8,128)S(1)} %cholesky.346), custom_call_target="Cholesky" | custom-call | tf_op jit(solution)/shard_map/jit(cholesky)/cholesky | solution.py:108
  100.3 9.8 %custom-call.40 = f32[1,128,128]{1,2,0:T(8,128)S(1)} custom-call(f32[1,128,128]{2,1,0:T(8,128)S(1)} %get-tuple-element.77), custom_call_target="InvertDiagBlocksLowerTriangular" | custom-call | tf_op jit(solution)/shard_map/jit(cholesky)/cholesky | solution.py:108
  112.0 11.7 %cholesky.310 = f32[128,128]{1,0:T(8,128)S(1)} custom-call(f32[128,128]{1,0:T(8,128)S(1)} %cholesky.351), custom_call_target="Cholesky" | custom-call | tf_op jit(solution)/shard_map/jit(cholesky)/cholesky | solution.py:108
  124.4 9.8 %custom-call.41 = f32[1,128,128]{1,2,0:T(8,128)S(1)} custom-call(f32[1,128,128]{2,1,0:T(8,128)S(1)} %get-tuple-element.74), custom_call_target="InvertDiagBlocksLowerTriangular" | custom-call | tf_op jit(solution)/shard_map/jit(cholesky)/cholesky | solution.py:108
  135.7 11.7 %cholesky.327 = f32[128,128]{1,0:T(8,128)S(1)} custom-call(f32[128,128]{1,0:T(8,128)S(1)} %convolution_subtract_fusion.6), custom_call_target="Cholesky" | custom-call | tf_op jit(solution)/shard_map/jit(cholesky)/cholesky | solution.py:108
  152.5 17.8 %while.1 = (s32[]{:T(128)}, f32[640,640]{1,0:T(8,128)}, s32[5,2]{0,1:T(2,128)S(1)}, f32[5,128,128]{2,1,0:T(8,128)}, s32[]{:T(128)}) while((s32[]{:T(128)}, f32[640,640]{1,0:T(8,128)}, s32[5,2]{0,1:T(2,128)S(1)}, f32[5,128,128]{2,1,0:T(8,128)}, s32[]{:T(128)}) %tuple.96), condition=%wide.while_cond, body=%wide.while_body.sunk | while | flops 2 | bytes 132705 | solution.py:109
  153.6 2.8 bitcast_dynamic-update-slice_fusion.2
  157.0 2.8 bitcast_dynamic-update-slice_fusion.2
  160.5 2.8 bitcast_dynamic-update-slice_fusion.2
  164.0 2.8 bitcast_dynamic-update-slice_fusion.2
  167.5 2.8 bitcast_dynamic-update-slice_fusion.2
  170.3 50.7 %custom-call.42 = f32[5,128,128]{1,2,0:T(8,128)} custom-call(f32[5,128,128]{2,1,0:T(8,128)} %get-tuple-element.10), custom_call_target="InvertDiagBlocksLowerTriangular" | custom-call | tf_op jit(solution)/shard_map/triangular_solve | solution.py:109
  234.1 4.7 collective-permute-start.11
  238.8 5.0 fusion.240
  245.7 4.4 collective-permute-start.13
  250.2 2.6 collective-permute-done.12
  256.4 3.3 collective-permute-done.14
  260.4 3.8 collective-permute-done.15
  264.9 4.4 collective-permute-start.17
  269.3 6.9 collective-permute-done.16
  285.3 26.6 %collective-permute-done.18 = f32[3,512,256]{2,1,0:T(8,128)S(1)} collective-permute-done((f32[3,512,256]{2,1,0:T(8,128)S(1)}, f32[3,512,256]{2,1,0:T(8,128)S(1)}, u32[]{:S(2)}, u32[]{:S(2)}) %collective-permute-start.18) | collective-permute-done | bytes 1572896 | tf_op jit(solution)/shard_map/ppermute | solution.py:21
  317.5 2.0 fusion.71
  321.4 2.9 multiply_reduce_fusion.4
  324.3 40.9 %all-reduce.1 = (f32[256]{0:T(256)S(1)}, f32[256]{0:T(256)S(1)}) all-reduce(f32[256]{0:T(256)S(1)} %get-tuple-element.12, f32[256]{0:T(256)S(1)} %get-tuple-element.11), channel_id=1, replica_groups=mesh['gx'=16,'gy'=2] {'gx','gy'}, use_global_device_ids=true, to_apply=%region_11.13 | all-reduce | flops 512 | bytes 4096 | tf_op jit(solution)/shard_map/psum | solution.py:61
  369.6 5.2 collective-permute-done.20
  374.7 4.8 collective-permute-done.21
  380.9 4.6 collective-permute-start.23
  391.3 4.1 collective-permute-start.25
  395.4 2.7 collective-permute-done.24
  398.2 4.4 collective-permute-start.26
  404.5 7.1 collective-permute-done.26
  412.3 3.5 collective-permute-done.27
  417.2 36.8 %psum.44 = f32[256]{0:T(256)S(1)} all-reduce(f32[256]{0:T(256)S(1)} %get-tuple-element.128), channel_id=1, replica_groups=mesh['gx'=16,'gy'=2] {'gx','gy'}, use_global_device_ids=true, to_apply=%region_15.17 | all-reduce | flops 256 | bytes 2048 | tf_op jit(solution)/shard_map/psum | solution.py:61
  455.2 4.4 collective-permute-start.29
  459.6 7.0 collective-permute-done.28
  466.7 4.3 collective-permute-start.30
  478.3 24.6 %collective-permute-done.30 = f32[3,512,256]{2,1,0:T(8,128)S(1)} collective-permute-done((f32[3,512,256]{2,1,0:T(8,128)S(1)}, f32[3,512,256]{2,1,0:T(8,128)S(1)}, u32[]{:S(2)}, u32[]{:S(2)}) %collective-permute-start.30) | collective-permute-done | bytes 1572896 | tf_op jit(solution)/shard_map/ppermute | solution.py:21
  512.3 2.8 multiply_reduce_fusion.2
  515.2 43.2 %psum.45 = f32[256]{0:T(256)S(1)} all-reduce(f32[256]{0:T(256)S(1)} %get-tuple-element.130), channel_id=1, replica_groups=mesh['gx'=16,'gy'=2] {'gx','gy'}, use_global_device_ids=true, to_apply=%region_17.19 | all-reduce | flops 256 | bytes 2048 | tf_op jit(solution)/shard_map/psum | solution.py:173
  562.8 5.2 collective-permute-done.32
  568.0 4.8 collective-permute-done.33
  574.2 4.6 collective-permute-start.35
  584.5 4.1 collective-permute-start.37
  588.7 2.7 collective-permute-done.36
  591.4 4.4 collective-permute-start.38
  597.8 6.8 collective-permute-done.38
  605.2 3.5 collective-permute-done.39
  609.4 36.9 %psum.46 = f32[256]{0:T(256)S(1)} all-reduce(f32[256]{0:T(256)S(1)} %get-tuple-element.132), channel_id=1, replica_groups=mesh['gx'=16,'gy'=2] {'gx','gy'}, use_global_device_ids=true, to_apply=%region_19.21 | all-reduce | flops 256 | bytes 2048 | tf_op jit(solution)/shard_map/psum | solution.py:61
  646.4 4.4 collective-permute-start.41
  650.8 7.0 collective-permute-done.40
  657.9 4.3 collective-permute-start.42
  669.3 25.0 %collective-permute-done.42 = f32[3,512,256]{2,1,0:T(8,128)S(1)} collective-permute-done((f32[3,512,256]{2,1,0:T(8,128)S(1)}, f32[3,512,256]{2,1,0:T(8,128)S(1)}, u32[]{:S(2)}, u32[]{:S(2)}) %collective-permute-start.42) | collective-permute-done | bytes 1572896 | tf_op jit(solution)/shard_map/ppermute | solution.py:21
  699.8 2.1 fusion.59
  703.8 2.1 multiply_reduce_fusion
  705.9 43.1 %psum.47 = f32[256]{0:T(256)S(1)} all-reduce(f32[256]{0:T(256)S(1)} %get-tuple-element.134), channel_id=1, replica_groups=mesh['gx'=16,'gy'=2] {'gx','gy'}, use_global_device_ids=true, to_apply=%region_21.23 | all-reduce | flops 256 | bytes 2048 | tf_op jit(solution)/shard_map/psum | solution.py:173
  (239 shorter events, 132.9 us)
Async XLA Ops:
  0.6 13.0 %copy-start.7 = (s32[1,1,128]{2,1,0:T(1,128)S(1)}, s32[1,1,128]{2,1,0:T(1,128)}, u32[]{:S(2)}) copy-start(s32[1,1,128]{2,1,0:T(1,128)} %param.9) | copy-start | bytes 1540
  0.6 19.3 %copy-start = (f32[1,1,512,256]{3,2,1,0:T(8,128)S(1)}, f32[1,1,512,256]{3,2,1,0:T(8,128)}, u32[]{:S(2)}) copy-start(f32[1,1,512,256]{3,2,1,0:T(8,128)} %param.6) | copy-start | bytes 1572868
  0.7 13.4 %collective-permute-start.4 = (s32[128]{0:T(128)}, s32[128]{0:T(128)S(1)}, u32[]{:S(2)}, u32[]{:S(2)}) collective-permute-start(s32[128]{0:T(128)} %bitcast.373), channel_id=1, source_target_pairs={{0,2},{2,4},{4,6},{6,8},{8,10},{10,12},{12,14},{14,16},{16,18},{18... | collective-permute-start | bytes 1544 | tf_op jit(solution)/shard_map/ppermute | solution.py:15
  1.2 12.8 %collective-permute-start.5 = (s32[128]{0:T(128)}, s32[128]{0:T(128)S(1)}, u32[]{:S(2)}, u32[]{:S(2)}) collective-permute-start(s32[128]{0:T(128)} %bitcast.374), channel_id=1, source_target_pairs={{0,30},{2,0},{4,2},{6,4},{8,6},{10,8},{12,10},{14,12},{16,14},{18,... | collective-permute-start | bytes 1544 | tf_op jit(solution)/shard_map/ppermute | solution.py:15
  7.0 16.5 %collective-permute-start = (f32[3,512]{1,0:T(4,128)S(1)}, f32[3,512]{1,0:T(4,128)S(1)}, u32[]{:S(2)}, u32[]{:S(2)}) collective-permute-start(f32[3,512]{1,0:T(4,128)S(1)} %get-tuple-element.110), channel_id=1, source_target_pairs={{0,2},{2,4},{4,6},{6,8},{8,10},{10,12},{12,14},{14,16},{16,18},{18... | collective-permute-start | bytes 18440 | tf_op jit(solution)/shard_map/ppermute | solution.py:15
  7.0 16.4 %collective-permute-start.1 = (f32[3,512]{1,0:T(4,128)S(1)}, f32[3,512]{1,0:T(4,128)S(1)}, u32[]{:S(2)}, u32[]{:S(2)}) collective-permute-start(f32[3,512]{1,0:T(4,128)S(1)} %get-tuple-element.110), channel_id=1, source_target_pairs={{0,30},{2,0},{4,2},{6,4},{8,6},{10,8},{12,10},{14,12},{16,14},{18,... | collective-permute-start | bytes 18440 | tf_op jit(solution)/shard_map/ppermute | solution.py:15
  14.1 6.7 collective-permute-start.7
  15.4 6.3 collective-permute-start.6
  23.5 208.1 %collective-permute-start.8 = (f32[3,128,256]{2,1,0:T(8,128)}, f32[3,128,256]{2,1,0:T(8,128)}, u32[]{:S(2)}, u32[]{:S(2)}) collective-permute-start(f32[3,128,256]{2,1,0:T(8,128)} %pad_maximum_fusion.3), channel_id=1, source_target_pairs={{0,30},{2,0},{4,2},{6,4},{8,6},{10,8},{12,10},{14,12},{16,14},{18,... | collective-permute-start | bytes 1179656 | tf_op jit(solution)/shard_map/ppermute | solution.py:15
  23.5 7.5 collective-permute-start.2
  27.2 5.7 collective-permute-start.3
  29.3 5.1 copy-start.6
  29.3 5.1 copy-start.8
  29.3 202.3 %collective-permute-start.9 = (f32[3,128,256]{2,1,0:T(8,128)}, f32[3,128,256]{2,1,0:T(8,128)}, u32[]{:S(2)}, u32[]{:S(2)}) collective-permute-start(f32[3,128,256]{2,1,0:T(8,128)} %pad_maximum_fusion.4), channel_id=1, source_target_pairs={{0,2},{2,4},{4,6},{6,8},{8,10},{10,12},{12,14},{14,16},{16,18},{18... | collective-permute-start | bytes 1179656 | tf_op jit(solution)/shard_map/ppermute | solution.py:15
  37.5 1.2 copy-start.4
  170.3 54.7 %copy-start.3 = (f32[640,640]{1,0:T(8,128)S(1)}, f32[640,640]{1,0:T(8,128)}, u32[]{:S(2)}) copy-start(f32[640,640]{1,0:T(8,128)} %fusion.25) | copy-start | bytes 4915204
  222.2 4.3 copy-start.5
  232.8 11.1 %collective-permute-start.10 = (f32[128,256]{1,0:T(8,128)S(1)}, f32[128,256]{1,0:T(8,128)S(1)}, u32[]{:S(2)}, u32[]{:S(2)}) collective-permute-start(f32[128,256]{1,0:T(8,128)S(1)} %get-tuple-element.60), channel_id=1, source_target_pairs={{1,0},{3,2},{5,4},{7,6},{9,8},{11,10},{13,12},{15,14},{17,16},{19,... | collective-permute-start | bytes 393224 | tf_op jit(solution)/shard_map/ppermute | solution.py:21
  234.1 9.8 %collective-permute-start.11 = (f32[128,256]{1,0:T(8,128)S(1)}, f32[128,256]{1,0:T(8,128)S(1)}, u32[]{:S(2)}, u32[]{:S(2)}) collective-permute-start(f32[128,256]{1,0:T(8,128)S(1)} %get-tuple-element.61), channel_id=1, source_target_pairs={{0,1},{2,3},{4,5},{6,7},{8,9},{10,11},{12,13},{14,15},{16,17},{18,... | collective-permute-start | bytes 393224 | tf_op jit(solution)/shard_map/ppermute | solution.py:21
  245.7 7.1 collective-permute-start.12
  245.7 7.1 collective-permute-start.13
  252.9 6.9 collective-permute-start.14
  254.5 9.7 %collective-permute-start.15 = (f32[3,128,256]{2,1,0:T(8,128)S(1)}, f32[3,128,256]{2,1,0:T(8,128)S(1)}, u32[]{:S(2)}, u32[]{:S(2)}) collective-permute-start(f32[3,128,256]{2,1,0:T(8,128)S(1)} %pad_maximum_fusion.5), channel_id=1, source_target_pairs={{1,0},{3,2},{5,4},{7,6},{9,8},{11,10},{13,12},{15,14},{17,16},{19,... | collective-permute-start | bytes 1179656 | tf_op jit(solution)/shard_map/ppermute | solution.py:21
  264.8 11.5 %collective-permute-start.16 = (f32[512,256]{1,0:T(8,128)S(1)}, f32[512,256]{1,0:T(8,128)S(1)}, u32[]{:S(2)}, u32[]{:S(2)}) collective-permute-start(f32[512,256]{1,0:T(8,128)S(1)} %convolution_add_fusion.5), channel_id=1, source_target_pairs={{0,2},{2,4},{4,6},{6,8},{8,10},{10,12},{12,14},{14,16},{16,18},{18... | collective-permute-start | bytes 1572872 | tf_op jit(solution)/shard_map/ppermute | solution.py:15
  264.9 11.4 %collective-permute-start.17 = (f32[512,256]{1,0:T(8,128)S(1)}, f32[512,256]{1,0:T(8,128)S(1)}, u32[]{:S(2)}, u32[]{:S(2)}) collective-permute-start(f32[512,256]{1,0:T(8,128)S(1)} %convolution_add_fusion.5), channel_id=1, source_target_pairs={{0,30},{2,0},{4,2},{6,4},{8,6},{10,8},{12,10},{14,12},{16,14},{18,... | collective-permute-start | bytes 1572872 | tf_op jit(solution)/shard_map/ppermute | solution.py:15
  276.4 35.5 %collective-permute-start.18 = (f32[3,512,256]{2,1,0:T(8,128)S(1)}, f32[3,512,256]{2,1,0:T(8,128)S(1)}, u32[]{:S(2)}, u32[]{:S(2)}) collective-permute-start(f32[3,512,256]{2,1,0:T(8,128)S(1)} %pad_maximum_fusion), channel_id=1, source_target_pairs={{0,1},{2,3},{4,5},{6,7},{8,9},{10,11},{12,13},{14,15},{16,17},{18,... | collective-permute-start | bytes 4718600 | tf_op jit(solution)/shard_map/ppermute | solution.py:21
  278.0 39.5 %collective-permute-start.19 = (f32[3,512,256]{2,1,0:T(8,128)S(1)}, f32[3,512,256]{2,1,0:T(8,128)S(1)}, u32[]{:S(2)}, u32[]{:S(2)}) collective-permute-start(f32[3,512,256]{2,1,0:T(8,128)S(1)} %pad_maximum_fusion), channel_id=1, source_target_pairs={{1,0},{3,2},{5,4},{7,6},{9,8},{11,10},{13,12},{15,14},{17,16},{19,... | collective-permute-start | bytes 4718600 | tf_op jit(solution)/shard_map/ppermute | solution.py:21
  368.9 5.8 collective-permute-start.20
  369.5 10.1 %collective-permute-start.21 = (f32[3,128,256]{2,1,0:T(8,128)S(1)}, f32[3,128,256]{2,1,0:T(8,128)S(1)}, u32[]{:S(2)}, u32[]{:S(2)}) collective-permute-start(f32[3,128,256]{2,1,0:T(8,128)S(1)} %pad_maximum_fusion.7), channel_id=1, source_target_pairs={{0,2},{2,4},{4,6},{6,8},{8,10},{10,12},{12,14},{14,16},{16,18},{18... | collective-permute-start | bytes 1179656 | tf_op jit(solution)/shard_map/ppermute | solution.py:15
  379.6 7.7 %collective-permute-start.22 = (f32[128,256]{1,0:T(8,128)S(1)}, f32[128,256]{1,0:T(8,128)S(1)}, u32[]{:S(2)}, u32[]{:S(2)}) collective-permute-start(f32[128,256]{1,0:T(8,128)S(1)} %get-tuple-element.49), channel_id=1, source_target_pairs={{1,0},{3,2},{5,4},{7,6},{9,8},{11,10},{13,12},{15,14},{17,16},{19,... | collective-permute-start | bytes 393224 | tf_op jit(solution)/shard_map/ppermute | solution.py:21
  380.9 8.2 %collective-permute-start.23 = (f32[128,256]{1,0:T(8,128)S(1)}, f32[128,256]{1,0:T(8,128)S(1)}, u32[]{:S(2)}, u32[]{:S(2)}) collective-permute-start(f32[128,256]{1,0:T(8,128)S(1)} %get-tuple-element.50), channel_id=1, source_target_pairs={{0,1},{2,3},{4,5},{6,7},{8,9},{10,11},{12,13},{14,15},{16,17},{18,... | collective-permute-start | bytes 393224 | tf_op jit(solution)/shard_map/ppermute | solution.py:21
  390.9 7.2 collective-permute-start.24
  391.3 6.8 collective-permute-start.25
  398.2 13.5 %collective-permute-start.26 = (f32[3,128,256]{2,1,0:T(8,128)S(1)}, f32[3,128,256]{2,1,0:T(8,128)S(1)}, u32[]{:S(2)}, u32[]{:S(2)}) collective-permute-start(f32[3,128,256]{2,1,0:T(8,128)S(1)} %pad_maximum_fusion.8), channel_id=1, source_target_pairs={{0,1},{2,3},{4,5},{6,7},{8,9},{10,11},{12,13},{14,15},{16,17},{18,... | collective-permute-start | bytes 1179656 | tf_op jit(solution)/shard_map/ppermute | solution.py:21
  402.6 13.2 %collective-permute-start.27 = (f32[3,128,256]{2,1,0:T(8,128)S(1)}, f32[3,128,256]{2,1,0:T(8,128)S(1)}, u32[]{:S(2)}, u32[]{:S(2)}) collective-permute-start(f32[3,128,256]{2,1,0:T(8,128)S(1)} %pad_maximum_fusion.8), channel_id=1, source_target_pairs={{1,0},{3,2},{5,4},{7,6},{9,8},{11,10},{13,12},{15,14},{17,16},{19,... | collective-permute-start | bytes 1179656 | tf_op jit(solution)/shard_map/ppermute | solution.py:21
  455.1 57.2 %copy-start.1 = (f32[512,256]{1,0:T(8,128)}, f32[512,256]{1,0:T(8,128)S(1)}, u32[]{:S(2)}) copy-start(f32[512,256]{1,0:T(8,128)S(1)} %multiply_add_fusion.1) | copy-start | bytes 1572868
  455.1 11.5 %collective-permute-start.28 = (f32[512,256]{1,0:T(8,128)S(1)}, f32[512,256]{1,0:T(8,128)S(1)}, u32[]{:S(2)}, u32[]{:S(2)}) collective-permute-start(f32[512,256]{1,0:T(8,128)S(1)} %multiply_add_fusion.1), channel_id=1, source_target_pairs={{0,2},{2,4},{4,6},{6,8},{8,10},{10,12},{12,14},{14,16},{16,18},{18... | collective-permute-start | bytes 1572872 | tf_op jit(solution)/shard_map/ppermute | solution.py:15
  455.2 11.4 %collective-permute-start.29 = (f32[512,256]{1,0:T(8,128)S(1)}, f32[512,256]{1,0:T(8,128)S(1)}, u32[]{:S(2)}, u32[]{:S(2)}) collective-permute-start(f32[512,256]{1,0:T(8,128)S(1)} %multiply_add_fusion.1), channel_id=1, source_target_pairs={{0,30},{2,0},{4,2},{6,4},{8,6},{10,8},{12,10},{14,12},{16,14},{18,... | collective-permute-start | bytes 1572872 | tf_op jit(solution)/shard_map/ppermute | solution.py:15
  466.7 36.1 %collective-permute-start.30 = (f32[3,512,256]{2,1,0:T(8,128)S(1)}, f32[3,512,256]{2,1,0:T(8,128)S(1)}, u32[]{:S(2)}, u32[]{:S(2)}) collective-permute-start(f32[3,512,256]{2,1,0:T(8,128)S(1)} %pad_maximum_fusion.1), channel_id=1, source_target_pairs={{0,1},{2,3},{4,5},{6,7},{8,9},{10,11},{12,13},{14,15},{16,17},{18,... | collective-permute-start | bytes 4718600 | tf_op jit(solution)/shard_map/ppermute | solution.py:21
  471.0 37.4 %collective-permute-start.31 = (f32[3,512,256]{2,1,0:T(8,128)S(1)}, f32[3,512,256]{2,1,0:T(8,128)S(1)}, u32[]{:S(2)}, u32[]{:S(2)}) collective-permute-start(f32[3,512,256]{2,1,0:T(8,128)S(1)} %pad_maximum_fusion.1), channel_id=1, source_target_pairs={{1,0},{3,2},{5,4},{7,6},{9,8},{11,10},{13,12},{15,14},{17,16},{19,... | collective-permute-start | bytes 4718600 | tf_op jit(solution)/shard_map/ppermute | solution.py:21
  562.1 5.9 collective-permute-start.32
  562.7 10.1 %collective-permute-start.33 = (f32[3,128,256]{2,1,0:T(8,128)S(1)}, f32[3,128,256]{2,1,0:T(8,128)S(1)}, u32[]{:S(2)}, u32[]{:S(2)}) collective-permute-start(f32[3,128,256]{2,1,0:T(8,128)S(1)} %pad_maximum_fusion.10), channel_id=1, source_target_pairs={{0,2},{2,4},{4,6},{6,8},{8,10},{10,12},{12,14},{14,16},{16,18},{18... | collective-permute-start | bytes 1179656 | tf_op jit(solution)/shard_map/ppermute | solution.py:15
  572.9 7.8 %collective-permute-start.34 = (f32[128,256]{1,0:T(8,128)S(1)}, f32[128,256]{1,0:T(8,128)S(1)}, u32[]{:S(2)}, u32[]{:S(2)}) collective-permute-start(f32[128,256]{1,0:T(8,128)S(1)} %get-tuple-element.38), channel_id=1, source_target_pairs={{1,0},{3,2},{5,4},{7,6},{9,8},{11,10},{13,12},{15,14},{17,16},{19,... | collective-permute-start | bytes 393224 | tf_op jit(solution)/shard_map/ppermute | solution.py:21
  574.2 8.2 %collective-permute-start.35 = (f32[128,256]{1,0:T(8,128)S(1)}, f32[128,256]{1,0:T(8,128)S(1)}, u32[]{:S(2)}, u32[]{:S(2)}) collective-permute-start(f32[128,256]{1,0:T(8,128)S(1)} %get-tuple-element.39), channel_id=1, source_target_pairs={{0,1},{2,3},{4,5},{6,7},{8,9},{10,11},{12,13},{14,15},{16,17},{18,... | collective-permute-start | bytes 393224 | tf_op jit(solution)/shard_map/ppermute | solution.py:21
  584.2 7.2 collective-permute-start.36
  584.5 6.9 collective-permute-start.37
  591.4 13.1 %collective-permute-start.38 = (f32[3,128,256]{2,1,0:T(8,128)S(1)}, f32[3,128,256]{2,1,0:T(8,128)S(1)}, u32[]{:S(2)}, u32[]{:S(2)}) collective-permute-start(f32[3,128,256]{2,1,0:T(8,128)S(1)} %pad_maximum_fusion.11), channel_id=1, source_target_pairs={{0,1},{2,3},{4,5},{6,7},{8,9},{10,11},{12,13},{14,15},{16,17},{18,... | collective-permute-start | bytes 1179656 | tf_op jit(solution)/shard_map/ppermute | solution.py:21
  595.9 12.8 %collective-permute-start.39 = (f32[3,128,256]{2,1,0:T(8,128)S(1)}, f32[3,128,256]{2,1,0:T(8,128)S(1)}, u32[]{:S(2)}, u32[]{:S(2)}) collective-permute-start(f32[3,128,256]{2,1,0:T(8,128)S(1)} %pad_maximum_fusion.11), channel_id=1, source_target_pairs={{1,0},{3,2},{5,4},{7,6},{9,8},{11,10},{13,12},{15,14},{17,16},{19,... | collective-permute-start | bytes 1179656 | tf_op jit(solution)/shard_map/ppermute | solution.py:21
  605.2 41.1 %copy-start.2 = (f32[512,256]{1,0:T(8,128)S(1)}, f32[512,256]{1,0:T(8,128)}, u32[]{:S(2)}) copy-start(f32[512,256]{1,0:T(8,128)} %copy-done.1) | copy-start | bytes 1572868
  646.3 11.5 %collective-permute-start.40 = (f32[512,256]{1,0:T(8,128)S(1)}, f32[512,256]{1,0:T(8,128)S(1)}, u32[]{:S(2)}, u32[]{:S(2)}) collective-permute-start(f32[512,256]{1,0:T(8,128)S(1)} %multiply_add_fusion), channel_id=1, source_target_pairs={{0,2},{2,4},{4,6},{6,8},{8,10},{10,12},{12,14},{14,16},{16,18},{18... | collective-permute-start | bytes 1572872 | tf_op jit(solution)/shard_map/ppermute | solution.py:15
  646.4 11.4 %collective-permute-start.41 = (f32[512,256]{1,0:T(8,128)S(1)}, f32[512,256]{1,0:T(8,128)S(1)}, u32[]{:S(2)}, u32[]{:S(2)}) collective-permute-start(f32[512,256]{1,0:T(8,128)S(1)} %multiply_add_fusion), channel_id=1, source_target_pairs={{0,30},{2,0},{4,2},{6,4},{8,6},{10,8},{12,10},{14,12},{16,14},{18,... | collective-permute-start | bytes 1572872 | tf_op jit(solution)/shard_map/ppermute | solution.py:15
  657.9 36.3 %collective-permute-start.42 = (f32[3,512,256]{2,1,0:T(8,128)S(1)}, f32[3,512,256]{2,1,0:T(8,128)S(1)}, u32[]{:S(2)}, u32[]{:S(2)}) collective-permute-start(f32[3,512,256]{2,1,0:T(8,128)S(1)} %pad_maximum_fusion.2), channel_id=1, source_target_pairs={{0,1},{2,3},{4,5},{6,7},{8,9},{10,11},{12,13},{14,15},{16,17},{18,... | collective-permute-start | bytes 4718600 | tf_op jit(solution)/shard_map/ppermute | solution.py:21
  662.2 37.6 %collective-permute-start.43 = (f32[3,512,256]{2,1,0:T(8,128)S(1)}, f32[3,512,256]{2,1,0:T(8,128)S(1)}, u32[]{:S(2)}, u32[]{:S(2)}) collective-permute-start(f32[3,512,256]{2,1,0:T(8,128)S(1)} %pad_maximum_fusion.2), channel_id=1, source_target_pairs={{1,0},{3,2},{5,4},{7,6},{9,8},{11,10},{13,12},{15,14},{17,16},{19,... | collective-permute-start | bytes 4718600 | tf_op jit(solution)/shard_map/ppermute | solution.py:21
where the time goes:
time: 756 us; the launch traced here: 751 us
  blocking collectives  201 us (27%)
  other arithmetic  168 us (22%)
  waiting for transfers between devices  161 us (21%)
  starting transfers between devices  96.9 us (13%)
  matrix products  94.8 us (13%)
  local copies, waits for them, and re-layouts  22.5 us (3%)
    psum x3, blocking collectives, residual_dot(): return lax.psum(column_sum(residue, precond), ('gx', 'gy'))  115 us
    ppermute x22, waiting for transfers between devices, passed_along(): return lax.ppermute(block, axis, route)  112 us
    another operation x19, other arithmetic, shards(): factor = jnp.linalg.cholesky(local_matrix)  101 us
    psum x2, blocking collectives, shards(): lax.psum(column_sum(direction, accumulated), ('gx', 'gy'))  86.3 us
    ppermute x22, starting transfers between devices, passed_along(): return lax.ppermute(block, axis, route)  57.9 us
    dot_general x27, matrix products, shards(): jnp.dot(kernel_block(own_pos, positions[operate_row_off][operate_col_off]...  52.9 us
    another operation x3, other arithmetic, shards(): lax.linalg.triangular_solve(factor, jnp.eye(ext_len, dtype=jnp.float32),...  52 us
    ppermute x22, waiting for transfers between devices, shifted(): lax.ppermute(value, axis, [(i, (i + by) % count) for i in range(count)])  49 us
  transfers between devices with their start and end apart: 44, of which 24 were waited for; matrix products, arithmetic and copies ran while one was open for 33% of the time, Pallas kernels for 0%

commit v1 on v0

--- a/solution.py
+++ b/solution.py
@@ -170,7 +170,7 @@
                     precision=HIGH,
                     preferred_element_type=jnp.float32,
                 )
-        step_size = inner_now / lax.psum(column_sum(direction, accumulated), ("gx", "gy"))
+        step_size = inner_now / lax.psum(lax.psum(column_sum(direction, accumulated), "gy"), "gx")
         solution = solution + step_size * direction
         residual = residual - step_size * accumulated
         if iteration + 1 < ITERS:

time: 756 us -> 777 us (1.028)
  blocking collectives: 201 us -> 229 us
  waiting for transfers between devices: 161 us -> 153 us
    psum x2 -> x6, blocking collectives: 86.3 us -> 116 us  [the longest x3 99.8 us: shards(): lax.psum(lax.psum(column_sum(direction, accumulated), 'gy'), 'gx')]
    ppermute x22, waiting for transfers between devices: 112 us -> 105 us  [passed_along(): return lax.ppermute(block, axis, route)]
  transfers between devices with their start and end apart: 44 -> 44, of which waited for: 24 -> 24; matrix products, arithmetic and copies ran while one was open for 33% -> 32% of each run, Pallas kernels for 0% -> 0%
where the time goes in v1:
time: 777 us; the launch traced here: 772 us
  blocking collectives  229 us (29%)
  other arithmetic  168 us (22%)
  waiting for transfers between devices  153 us (20%)
  starting transfers between devices  99.2 us (13%)
  matrix products  94.8 us (12%)
  local copies, waits for them, and re-layouts  22.7 us (3%)
    psum x3, blocking collectives, residual_dot(): return lax.psum(column_sum(residue, precond), ('gx', 'gy'))  113 us
    ppermute x22, waiting for transfers between devices, passed_along(): return lax.ppermute(block, axis, route)  105 us
    another operation x19, other arithmetic, shards(): factor = jnp.linalg.cholesky(local_matrix)  101 us
    psum x3, blocking collectives, shards(): lax.psum(lax.psum(column_sum(direction, accumulated), 'gy'), 'gx')  99.8 us
    ppermute x22, starting transfers between devices, passed_along(): return lax.ppermute(block, axis, route)  57.9 us
    dot_general x27, matrix products, shards(): jnp.dot(kernel_block(own_pos, positions[operate_row_off][operate_col_off]...  52.9 us
    another operation x3, other arithmetic, shards(): lax.linalg.triangular_solve(factor, jnp.eye(ext_len, dtype=jnp.float32),...  52 us
    ppermute x22, waiting for transfers between devices, shifted(): lax.ppermute(value, axis, [(i, (i + by) % count) for i in range(count)])  48.2 us
  transfers between devices with their start and end apart: 44, of which 24 were waited for; matrix products, arithmetic and copies ran while one was open for 32% of the time, Pallas kernels for 0%

profile of v1, /device:TPU:0, one launch (start us, length us, event | category | flops | bytes accessed | tf_op | source)
XLA Modules:
  0.0 772.3 jit_solution(13430832872647176282)
XLA Ops:
  1.2 5.0 collective-permute-start.5
  7.0 4.4 collective-permute-start.1
  15.4 4.5 collective-permute-start.6
  23.5 3.7 collective-permute-start.2
  34.4 3.1 add_multiply_fusion
  38.7 11.7 %cholesky.132 = f32[128,128]{1,0:T(8,128)S(1)} custom-call(f32[128,128]{1,0:T(8,128)S(1)} %cholesky.337), custom_call_target="Cholesky" | custom-call | tf_op jit(solution)/shard_map/jit(cholesky)/cholesky | solution.py:108
  50.5 9.8 %custom-call.38 = f32[1,128,128]{1,2,0:T(8,128)S(1)} custom-call(f32[1,128,128]{2,1,0:T(8,128)S(1)} %get-tuple-element.81), custom_call_target="InvertDiagBlocksLowerTriangular" | custom-call | tf_op jit(solution)/shard_map/jit(cholesky)/cholesky | solution.py:108
  63.0 11.9 %cholesky.270 = f32[128,128]{1,0:T(8,128)S(1)} custom-call(f32[128,128]{1,0:T(8,128)S(1)} %cholesky.341), custom_call_target="Cholesky" | custom-call | tf_op jit(solution)/shard_map/jit(cholesky)/cholesky | solution.py:108
  76.3 9.8 %custom-call.39 = f32[1,128,128]{1,2,0:T(8,128)S(1)} custom-call(f32[1,128,128]{2,1,0:T(8,128)S(1)} %get-tuple-element.78), custom_call_target="InvertDiagBlocksLowerTriangular" | custom-call | tf_op jit(solution)/shard_map/jit(cholesky)/cholesky | solution.py:108
  87.8 11.7 %cholesky.291 = f32[128,128]{1,0:T(8,128)S(1)} custom-call(f32[128,128]{1,0:T(8,128)S(1)} %cholesky.346), custom_call_target="Cholesky" | custom-call | tf_op jit(solution)/shard_map/jit(cholesky)/cholesky | solution.py:108
  100.2 9.8 %custom-call.40 = f32[1,128,128]{1,2,0:T(8,128)S(1)} custom-call(f32[1,128,128]{2,1,0:T(8,128)S(1)} %get-tuple-element.75), custom_call_target="InvertDiagBlocksLowerTriangular" | custom-call | tf_op jit(solution)/shard_map/jit(cholesky)/cholesky | solution.py:108
  111.9 11.7 %cholesky.310 = f32[128,128]{1,0:T(8,128)S(1)} custom-call(f32[128,128]{1,0:T(8,128)S(1)} %cholesky.351), custom_call_target="Cholesky" | custom-call | tf_op jit(solution)/shard_map/jit(cholesky)/cholesky | solution.py:108
  124.3 9.8 %custom-call.41 = f32[1,128,128]{1,2,0:T(8,128)S(1)} custom-call(f32[1,128,128]{2,1,0:T(8,128)S(1)} %get-tuple-element.72), custom_call_target="InvertDiagBlocksLowerTriangular" | custom-call | tf_op jit(solution)/shard_map/jit(cholesky)/cholesky | solution.py:108
  135.6 11.7 %cholesky.327 = f32[128,128]{1,0:T(8,128)S(1)} custom-call(f32[128,128]{1,0:T(8,128)S(1)} %convolution_subtract_fusion.6), custom_call_target="Cholesky" | custom-call | tf_op jit(solution)/shard_map/jit(cholesky)/cholesky | solution.py:108
  152.2 18.0 %while.1 = (s32[]{:T(128)}, f32[640,640]{1,0:T(8,128)}, s32[5,2]{0,1:T(2,128)S(1)}, f32[5,128,128]{2,1,0:T(8,128)}, s32[]{:T(128)}) while((s32[]{:T(128)}, f32[640,640]{1,0:T(8,128)}, s32[5,2]{0,1:T(2,128)S(1)}, f32[5,128,128]{2,1,0:T(8,128)}, s32[]{:T(128)}) %tuple.96), condition=%wide.while_cond, body=%wide.while_body.sunk | while | flops 2 | bytes 132705 | solution.py:109
  153.3 2.9 bitcast_dynamic-update-slice_fusion.2
  156.8 2.9 bitcast_dynamic-update-slice_fusion.2
  160.3 2.9 bitcast_dynamic-update-slice_fusion.2
  163.8 2.9 bitcast_dynamic-update-slice_fusion.2
  167.4 2.8 bitcast_dynamic-update-slice_fusion.2
  170.2 50.7 %custom-call.42 = f32[5,128,128]{1,2,0:T(8,128)} custom-call(f32[5,128,128]{2,1,0:T(8,128)} %get-tuple-element.10), custom_call_target="InvertDiagBlocksLowerTriangular" | custom-call | tf_op jit(solution)/shard_map/triangular_solve | solution.py:109
  234.0 4.7 collective-permute-start.11
  238.7 5.0 fusion.240
  245.6 4.4 collective-permute-start.13
  250.1 2.6 collective-permute-done.12
  256.3 3.3 collective-permute-done.14
  260.2 3.8 collective-permute-done.15
  264.7 4.4 collective-permute-start.17
  269.2 6.9 collective-permute-done.16
  285.2 26.6 %collective-permute-done.18 = f32[3,512,256]{2,1,0:T(8,128)S(1)} collective-permute-done((f32[3,512,256]{2,1,0:T(8,128)S(1)}, f32[3,512,256]{2,1,0:T(8,128)S(1)}, u32[]{:S(2)}, u32[]{:S(2)}) %collective-permute-start.18) | collective-permute-done | bytes 1572896 | tf_op jit(solution)/shard_map/ppermute | solution.py:21
  321.2 2.9 multiply_reduce_fusion.4
  324.1 5.4 psum.64
  329.5 32.1 %psum.65 = f32[256]{0:T(256)S(1)} all-reduce(f32[256]{0:T(256)S(1)} %psum.64), channel_id=1, replica_groups=mesh['gx'=16,'gy'=2] {'gx'}, use_global_device_ids=true, to_apply=%region_14.16 | all-reduce | flops 256 | bytes 2048 | tf_op jit(solution)/shard_map/psum | solution.py:173
  361.6 36.9 %psum.63 = f32[256]{0:T(256)S(1)} all-reduce(f32[256]{0:T(256)S(1)} %get-tuple-element.12), channel_id=1, replica_groups=mesh['gx'=16,'gy'=2] {'gx','gy'}, use_global_device_ids=true, to_apply=%region_11.13 | all-reduce | flops 256 | bytes 2048 | tf_op jit(solution)/shard_map/psum | solution.py:61
  402.1 2.9 collective-permute-start.20
  405.2 5.2 collective-permute-done.20
  410.4 4.7 collective-permute-done.21
  416.4 4.6 collective-permute-start.23
  425.3 4.4 collective-permute-start.25
  432.5 4.4 collective-permute-start.26
  438.8 4.9 collective-permute-done.26
  444.3 3.5 collective-permute-done.27
  449.2 39.0 %psum.66 = f32[256]{0:T(256)S(1)} all-reduce(f32[256]{0:T(256)S(1)} %get-tuple-element.126), channel_id=1, replica_groups=mesh['gx'=16,'gy'=2] {'gx','gy'}, use_global_device_ids=true, to_apply=%region_16.18 | all-reduce | flops 256 | bytes 2048 | tf_op jit(solution)/shard_map/psum | solution.py:61
  489.5 4.4 collective-permute-start.29
  493.9 7.0 collective-permute-done.28
  501.0 4.3 collective-permute-start.30
  512.6 23.4 %collective-permute-done.30 = f32[3,512,256]{2,1,0:T(8,128)S(1)} collective-permute-done((f32[3,512,256]{2,1,0:T(8,128)S(1)}, f32[3,512,256]{2,1,0:T(8,128)S(1)}, u32[]{:S(2)}, u32[]{:S(2)}) %collective-permute-start.30) | collective-permute-done | bytes 1572896 | tf_op jit(solution)/shard_map/ppermute | solution.py:21
  545.5 2.8 multiply_reduce_fusion.2
  548.3 5.4 psum.67
  553.7 33.9 %psum.68 = f32[256]{0:T(256)S(1)} all-reduce(f32[256]{0:T(256)S(1)} %psum.67), channel_id=1, replica_groups=mesh['gx'=16,'gy'=2] {'gx'}, use_global_device_ids=true, to_apply=%region_19.21 | all-reduce | flops 256 | bytes 2048 | tf_op jit(solution)/shard_map/psum | solution.py:173
  592.0 4.7 collective-permute-done.32
  596.7 4.8 collective-permute-done.33
  602.9 4.6 collective-permute-start.35
  612.1 4.4 collective-permute-start.37
  619.2 4.4 collective-permute-start.38
  625.6 3.6 collective-permute-done.38
  629.8 3.5 collective-permute-done.39
  634.0 37.2 %psum.69 = f32[256]{0:T(256)S(1)} all-reduce(f32[256]{0:T(256)S(1)} %get-tuple-element.130), channel_id=1, replica_groups=mesh['gx'=16,'gy'=2] {'gx','gy'}, use_global_device_ids=true, to_apply=%region_21.23 | all-reduce | flops 256 | bytes 2048 | tf_op jit(solution)/shard_map/psum | solution.py:61
  671.4 4.4 collective-permute-start.41
  675.8 7.0 collective-permute-done.40
  682.9 4.3 collective-permute-start.42
  694.3 25.6 %collective-permute-done.42 = f32[3,512,256]{2,1,0:T(8,128)S(1)} collective-permute-done((f32[3,512,256]{2,1,0:T(8,128)S(1)}, f32[3,512,256]{2,1,0:T(8,128)S(1)}, u32[]{:S(2)}, u32[]{:S(2)}) %collective-permute-start.42) | collective-permute-done | bytes 1572896 | tf_op jit(solution)/shard_map/ppermute | solution.py:21
  731.5 5.4 psum.70
  736.9 33.8 %psum.71 = f32[256]{0:T(256)S(1)} all-reduce(f32[256]{0:T(256)S(1)} %psum.70), channel_id=1, replica_groups=mesh['gx'=16,'gy'=2] {'gx'}, use_global_device_ids=true, to_apply=%region_24.26 | all-reduce | flops 256 | bytes 2048 | tf_op jit(solution)/shard_map/psum | solution.py:173
  (243 shorter events, 141.1 us)
Async XLA Ops:
  0.6 12.9 %copy-start.7 = (s32[1,1,128]{2,1,0:T(1,128)S(1)}, s32[1,1,128]{2,1,0:T(1,128)}, u32[]{:S(2)}) copy-start(s32[1,1,128]{2,1,0:T(1,128)} %param.9) | copy-start | bytes 1540
  0.6 19.3 %copy-start = (f32[1,1,512,256]{3,2,1,0:T(8,128)S(1)}, f32[1,1,512,256]{3,2,1,0:T(8,128)}, u32[]{:S(2)}) copy-start(f32[1,1,512,256]{3,2,1,0:T(8,128)} %param.6) | copy-start | bytes 1572868
  0.7 13.4 %collective-permute-start.4 = (s32[128]{0:T(128)}, s32[128]{0:T(128)S(1)}, u32[]{:S(2)}, u32[]{:S(2)}) collective-permute-start(s32[128]{0:T(128)} %bitcast.373), channel_id=1, source_target_pairs={{0,2},{2,4},{4,6},{6,8},{8,10},{10,12},{12,14},{14,16},{16,18},{18... | collective-permute-start | bytes 1544 | tf_op jit(solution)/shard_map/ppermute | solution.py:15
  1.2 12.8 %collective-permute-start.5 = (s32[128]{0:T(128)}, s32[128]{0:T(128)S(1)}, u32[]{:S(2)}, u32[]{:S(2)}) collective-permute-start(s32[128]{0:T(128)} %bitcast.374), channel_id=1, source_target_pairs={{0,30},{2,0},{4,2},{6,4},{8,6},{10,8},{12,10},{14,12},{16,14},{18,... | collective-permute-start | bytes 1544 | tf_op jit(solution)/shard_map/ppermute | solution.py:15
  7.0 16.5 %collective-permute-start = (f32[3,512]{1,0:T(4,128)S(1)}, f32[3,512]{1,0:T(4,128)S(1)}, u32[]{:S(2)}, u32[]{:S(2)}) collective-permute-start(f32[3,512]{1,0:T(4,128)S(1)} %get-tuple-element.108), channel_id=1, source_target_pairs={{0,2},{2,4},{4,6},{6,8},{8,10},{10,12},{12,14},{14,16},{16,18},{18... | collective-permute-start | bytes 18440 | tf_op jit(solution)/shard_map/ppermute | solution.py:15
  7.0 16.4 %collective-permute-start.1 = (f32[3,512]{1,0:T(4,128)S(1)}, f32[3,512]{1,0:T(4,128)S(1)}, u32[]{:S(2)}, u32[]{:S(2)}) collective-permute-start(f32[3,512]{1,0:T(4,128)S(1)} %get-tuple-element.108), channel_id=1, source_target_pairs={{0,30},{2,0},{4,2},{6,4},{8,6},{10,8},{12,10},{14,12},{16,14},{18,... | collective-permute-start | bytes 18440 | tf_op jit(solution)/shard_map/ppermute | solution.py:15
  14.1 6.7 collective-permute-start.7
  15.4 6.3 collective-permute-start.6
  23.4 208.0 %collective-permute-start.8 = (f32[3,128,256]{2,1,0:T(8,128)}, f32[3,128,256]{2,1,0:T(8,128)}, u32[]{:S(2)}, u32[]{:S(2)}) collective-permute-start(f32[3,128,256]{2,1,0:T(8,128)} %pad_maximum_fusion.3), channel_id=1, source_target_pairs={{0,30},{2,0},{4,2},{6,4},{8,6},{10,8},{12,10},{14,12},{16,14},{18,... | collective-permute-start | bytes 1179656 | tf_op jit(solution)/shard_map/ppermute | solution.py:15
  23.5 7.5 collective-permute-start.2
  27.2 5.7 collective-permute-start.3
  29.3 5.1 copy-start.6
  29.3 5.1 copy-start.8
  29.3 202.2 %collective-permute-start.9 = (f32[3,128,256]{2,1,0:T(8,128)}, f32[3,128,256]{2,1,0:T(8,128)}, u32[]{:S(2)}, u32[]{:S(2)}) collective-permute-start(f32[3,128,256]{2,1,0:T(8,128)} %pad_maximum_fusion.4), channel_id=1, source_target_pairs={{0,2},{2,4},{4,6},{6,8},{8,10},{10,12},{12,14},{14,16},{16,18},{18... | collective-permute-start | bytes 1179656 | tf_op jit(solution)/shard_map/ppermute | solution.py:15
  37.5 1.2 copy-start.4
  170.2 54.7 %copy-start.3 = (f32[640,640]{1,0:T(8,128)S(1)}, f32[640,640]{1,0:T(8,128)}, u32[]{:S(2)}) copy-start(f32[640,640]{1,0:T(8,128)} %fusion.25) | copy-start | bytes 4915204
  222.1 4.2 copy-start.5
  232.7 11.1 %collective-permute-start.10 = (f32[128,256]{1,0:T(8,128)S(1)}, f32[128,256]{1,0:T(8,128)S(1)}, u32[]{:S(2)}, u32[]{:S(2)}) collective-permute-start(f32[128,256]{1,0:T(8,128)S(1)} %get-tuple-element.58), channel_id=1, source_target_pairs={{1,0},{3,2},{5,4},{7,6},{9,8},{11,10},{13,12},{15,14},{17,16},{19,... | collective-permute-start | bytes 393224 | tf_op jit(solution)/shard_map/ppermute | solution.py:21
  234.0 9.8 %collective-permute-start.11 = (f32[128,256]{1,0:T(8,128)S(1)}, f32[128,256]{1,0:T(8,128)S(1)}, u32[]{:S(2)}, u32[]{:S(2)}) collective-permute-start(f32[128,256]{1,0:T(8,128)S(1)} %get-tuple-element.59), channel_id=1, source_target_pairs={{0,1},{2,3},{4,5},{6,7},{8,9},{10,11},{12,13},{14,15},{16,17},{18,... | collective-permute-start | bytes 393224 | tf_op jit(solution)/shard_map/ppermute | solution.py:21
  245.6 7.1 collective-permute-start.12
  245.6 7.1 collective-permute-start.13
  252.7 6.9 collective-permute-start.14
  254.4 9.7 %collective-permute-start.15 = (f32[3,128,256]{2,1,0:T(8,128)S(1)}, f32[3,128,256]{2,1,0:T(8,128)S(1)}, u32[]{:S(2)}, u32[]{:S(2)}) collective-permute-start(f32[3,128,256]{2,1,0:T(8,128)S(1)} %pad_maximum_fusion.5), channel_id=1, source_target_pairs={{1,0},{3,2},{5,4},{7,6},{9,8},{11,10},{13,12},{15,14},{17,16},{19,... | collective-permute-start | bytes 1179656 | tf_op jit(solution)/shard_map/ppermute | solution.py:21
  264.7 11.5 %collective-permute-start.16 = (f32[512,256]{1,0:T(8,128)S(1)}, f32[512,256]{1,0:T(8,128)S(1)}, u32[]{:S(2)}, u32[]{:S(2)}) collective-permute-start(f32[512,256]{1,0:T(8,128)S(1)} %convolution_add_fusion.5), channel_id=1, source_target_pairs={{0,2},{2,4},{4,6},{6,8},{8,10},{10,12},{12,14},{14,16},{16,18},{18... | collective-permute-start | bytes 1572872 | tf_op jit(solution)/shard_map/ppermute | solution.py:15
  264.7 11.4 %collective-permute-start.17 = (f32[512,256]{1,0:T(8,128)S(1)}, f32[512,256]{1,0:T(8,128)S(1)}, u32[]{:S(2)}, u32[]{:S(2)}) collective-permute-start(f32[512,256]{1,0:T(8,128)S(1)} %convolution_add_fusion.5), channel_id=1, source_target_pairs={{0,30},{2,0},{4,2},{6,4},{8,6},{10,8},{12,10},{14,12},{16,14},{18,... | collective-permute-start | bytes 1572872 | tf_op jit(solution)/shard_map/ppermute | solution.py:15
  276.3 35.5 %collective-permute-start.18 = (f32[3,512,256]{2,1,0:T(8,128)S(1)}, f32[3,512,256]{2,1,0:T(8,128)S(1)}, u32[]{:S(2)}, u32[]{:S(2)}) collective-permute-start(f32[3,512,256]{2,1,0:T(8,128)S(1)} %pad_maximum_fusion), channel_id=1, source_target_pairs={{0,1},{2,3},{4,5},{6,7},{8,9},{10,11},{12,13},{14,15},{16,17},{18,... | collective-permute-start | bytes 4718600 | tf_op jit(solution)/shard_map/ppermute | solution.py:21
  277.9 39.5 %collective-permute-start.19 = (f32[3,512,256]{2,1,0:T(8,128)S(1)}, f32[3,512,256]{2,1,0:T(8,128)S(1)}, u32[]{:S(2)}, u32[]{:S(2)}) collective-permute-start(f32[3,512,256]{2,1,0:T(8,128)S(1)} %pad_maximum_fusion), channel_id=1, source_target_pairs={{1,0},{3,2},{5,4},{7,6},{9,8},{11,10},{13,12},{15,14},{17,16},{19,... | collective-permute-start | bytes 4718600 | tf_op jit(solution)/shard_map/ppermute | solution.py:21
  402.1 8.2 %collective-permute-start.20 = (f32[3,128,256]{2,1,0:T(8,128)S(1)}, f32[3,128,256]{2,1,0:T(8,128)S(1)}, u32[]{:S(2)}, u32[]{:S(2)}) collective-permute-start(f32[3,128,256]{2,1,0:T(8,128)S(1)} %pad_maximum_fusion.6), channel_id=1, source_target_pairs={{0,30},{2,0},{4,2},{6,4},{8,6},{10,8},{12,10},{14,12},{16,14},{18,... | collective-permute-start | bytes 1179656 | tf_op jit(solution)/shard_map/ppermute | solution.py:15
  405.1 10.0 %collective-permute-start.21 = (f32[3,128,256]{2,1,0:T(8,128)S(1)}, f32[3,128,256]{2,1,0:T(8,128)S(1)}, u32[]{:S(2)}, u32[]{:S(2)}) collective-permute-start(f32[3,128,256]{2,1,0:T(8,128)S(1)} %pad_maximum_fusion.7), channel_id=1, source_target_pairs={{0,2},{2,4},{4,6},{6,8},{8,10},{10,12},{12,14},{14,16},{16,18},{18... | collective-permute-start | bytes 1179656 | tf_op jit(solution)/shard_map/ppermute | solution.py:15
  415.1 6.9 collective-permute-start.22
  416.4 7.1 collective-permute-start.23
  425.3 7.1 collective-permute-start.24
  425.3 7.1 collective-permute-start.25
  432.5 11.2 %collective-permute-start.26 = (f32[3,128,256]{2,1,0:T(8,128)S(1)}, f32[3,128,256]{2,1,0:T(8,128)S(1)}, u32[]{:S(2)}, u32[]{:S(2)}) collective-permute-start(f32[3,128,256]{2,1,0:T(8,128)S(1)} %pad_maximum_fusion.8), channel_id=1, source_target_pairs={{0,1},{2,3},{4,5},{6,7},{8,9},{10,11},{12,13},{14,15},{16,17},{18,... | collective-permute-start | bytes 1179656 | tf_op jit(solution)/shard_map/ppermute | solution.py:21
  436.8 11.0 %collective-permute-start.27 = (f32[3,128,256]{2,1,0:T(8,128)S(1)}, f32[3,128,256]{2,1,0:T(8,128)S(1)}, u32[]{:S(2)}, u32[]{:S(2)}) collective-permute-start(f32[3,128,256]{2,1,0:T(8,128)S(1)} %pad_maximum_fusion.8), channel_id=1, source_target_pairs={{1,0},{3,2},{5,4},{7,6},{9,8},{11,10},{13,12},{15,14},{17,16},{19,... | collective-permute-start | bytes 1179656 | tf_op jit(solution)/shard_map/ppermute | solution.py:21
  489.4 56.1 %copy-start.1 = (f32[512,256]{1,0:T(8,128)}, f32[512,256]{1,0:T(8,128)S(1)}, u32[]{:S(2)}) copy-start(f32[512,256]{1,0:T(8,128)S(1)} %multiply_add_fusion.1) | copy-start | bytes 1572868
  489.4 11.5 %collective-permute-start.28 = (f32[512,256]{1,0:T(8,128)S(1)}, f32[512,256]{1,0:T(8,128)S(1)}, u32[]{:S(2)}, u32[]{:S(2)}) collective-permute-start(f32[512,256]{1,0:T(8,128)S(1)} %multiply_add_fusion.1), channel_id=1, source_target_pairs={{0,2},{2,4},{4,6},{6,8},{8,10},{10,12},{12,14},{14,16},{16,18},{18... | collective-permute-start | bytes 1572872 | tf_op jit(solution)/shard_map/ppermute | solution.py:15
  489.5 11.4 %collective-permute-start.29 = (f32[512,256]{1,0:T(8,128)S(1)}, f32[512,256]{1,0:T(8,128)S(1)}, u32[]{:S(2)}, u32[]{:S(2)}) collective-permute-start(f32[512,256]{1,0:T(8,128)S(1)} %multiply_add_fusion.1), channel_id=1, source_target_pairs={{0,30},{2,0},{4,2},{6,4},{8,6},{10,8},{12,10},{14,12},{16,14},{18,... | collective-permute-start | bytes 1572872 | tf_op jit(solution)/shard_map/ppermute | solution.py:15
  501.0 35.0 %collective-permute-start.30 = (f32[3,512,256]{2,1,0:T(8,128)S(1)}, f32[3,512,256]{2,1,0:T(8,128)S(1)}, u32[]{:S(2)}, u32[]{:S(2)}) collective-permute-start(f32[3,512,256]{2,1,0:T(8,128)S(1)} %pad_maximum_fusion.1), channel_id=1, source_target_pairs={{0,1},{2,3},{4,5},{6,7},{8,9},{10,11},{12,13},{14,15},{16,17},{18,... | collective-permute-start | bytes 4718600 | tf_op jit(solution)/shard_map/ppermute | solution.py:21
  505.3 36.3 %collective-permute-start.31 = (f32[3,512,256]{2,1,0:T(8,128)S(1)}, f32[3,512,256]{2,1,0:T(8,128)S(1)}, u32[]{:S(2)}, u32[]{:S(2)}) collective-permute-start(f32[3,512,256]{2,1,0:T(8,128)S(1)} %pad_maximum_fusion.1), channel_id=1, source_target_pairs={{1,0},{3,2},{5,4},{7,6},{9,8},{11,10},{13,12},{15,14},{17,16},{19,... | collective-permute-start | bytes 4718600 | tf_op jit(solution)/shard_map/ppermute | solution.py:21
  591.3 5.4 collective-permute-start.32
  591.4 10.1 %collective-permute-start.33 = (f32[3,128,256]{2,1,0:T(8,128)S(1)}, f32[3,128,256]{2,1,0:T(8,128)S(1)}, u32[]{:S(2)}, u32[]{:S(2)}) collective-permute-start(f32[3,128,256]{2,1,0:T(8,128)S(1)} %pad_maximum_fusion.10), channel_id=1, source_target_pairs={{0,2},{2,4},{4,6},{6,8},{8,10},{10,12},{12,14},{14,16},{16,18},{18... | collective-permute-start | bytes 1179656 | tf_op jit(solution)/shard_map/ppermute | solution.py:15
  601.6 7.5 collective-permute-start.34
  602.9 7.4 collective-permute-start.35
  612.0 7.1 collective-permute-start.36
  612.1 7.1 collective-permute-start.37
  619.2 9.9 %collective-permute-start.38 = (f32[3,128,256]{2,1,0:T(8,128)S(1)}, f32[3,128,256]{2,1,0:T(8,128)S(1)}, u32[]{:S(2)}, u32[]{:S(2)}) collective-permute-start(f32[3,128,256]{2,1,0:T(8,128)S(1)} %pad_maximum_fusion.11), channel_id=1, source_target_pairs={{0,1},{2,3},{4,5},{6,7},{8,9},{10,11},{12,13},{14,15},{16,17},{18,... | collective-permute-start | bytes 1179656 | tf_op jit(solution)/shard_map/ppermute | solution.py:21
  623.6 9.7 %collective-permute-start.39 = (f32[3,128,256]{2,1,0:T(8,128)S(1)}, f32[3,128,256]{2,1,0:T(8,128)S(1)}, u32[]{:S(2)}, u32[]{:S(2)}) collective-permute-start(f32[3,128,256]{2,1,0:T(8,128)S(1)} %pad_maximum_fusion.11), channel_id=1, source_target_pairs={{1,0},{3,2},{5,4},{7,6},{9,8},{11,10},{13,12},{15,14},{17,16},{19,... | collective-permute-start | bytes 1179656 | tf_op jit(solution)/shard_map/ppermute | solution.py:21
  629.8 41.5 %copy-start.2 = (f32[512,256]{1,0:T(8,128)S(1)}, f32[512,256]{1,0:T(8,128)}, u32[]{:S(2)}) copy-start(f32[512,256]{1,0:T(8,128)} %copy-done.1) | copy-start | bytes 1572868
  671.3 11.5 %collective-permute-start.40 = (f32[512,256]{1,0:T(8,128)S(1)}, f32[512,256]{1,0:T(8,128)S(1)}, u32[]{:S(2)}, u32[]{:S(2)}) collective-permute-start(f32[512,256]{1,0:T(8,128)S(1)} %multiply_add_fusion), channel_id=1, source_target_pairs={{0,2},{2,4},{4,6},{6,8},{8,10},{10,12},{12,14},{14,16},{16,18},{18... | collective-permute-start | bytes 1572872 | tf_op jit(solution)/shard_map/ppermute | solution.py:15
  671.4 11.4 %collective-permute-start.41 = (f32[512,256]{1,0:T(8,128)S(1)}, f32[512,256]{1,0:T(8,128)S(1)}, u32[]{:S(2)}, u32[]{:S(2)}) collective-permute-start(f32[512,256]{1,0:T(8,128)S(1)} %multiply_add_fusion), channel_id=1, source_target_pairs={{0,30},{2,0},{4,2},{6,4},{8,6},{10,8},{12,10},{14,12},{16,14},{18,... | collective-permute-start | bytes 1572872 | tf_op jit(solution)/shard_map/ppermute | solution.py:15
  682.9 37.0 %collective-permute-start.42 = (f32[3,512,256]{2,1,0:T(8,128)S(1)}, f32[3,512,256]{2,1,0:T(8,128)S(1)}, u32[]{:S(2)}, u32[]{:S(2)}) collective-permute-start(f32[3,512,256]{2,1,0:T(8,128)S(1)} %pad_maximum_fusion.2), channel_id=1, source_target_pairs={{0,1},{2,3},{4,5},{6,7},{8,9},{10,11},{12,13},{14,15},{16,17},{18,... | collective-permute-start | bytes 4718600 | tf_op jit(solution)/shard_map/ppermute | solution.py:21
  687.2 38.3 %collective-permute-start.43 = (f32[3,512,256]{2,1,0:T(8,128)S(1)}, f32[3,512,256]{2,1,0:T(8,128)S(1)}, u32[]{:S(2)}, u32[]{:S(2)}) collective-permute-start(f32[3,512,256]{2,1,0:T(8,128)S(1)} %pad_maximum_fusion.2), channel_id=1, source_target_pairs={{1,0},{3,2},{5,4},{7,6},{9,8},{11,10},{13,12},{15,14},{17,16},{19,... | collective-permute-start | bytes 4718600 | tf_op jit(solution)/shard_map/ppermute | solution.py:21
